TPU v7x, 32 devices: a whole 2x2x4 slice. The times are simulated.
32 devices in a mesh: groups: 2 (over y), dom: 4 (over z), sub: 2 (over x), field: 2 (over core).
Axes of the slice: x: 2, y: 2, z: 4, core: 2. Of those that a mesh axis runs over, the one named last changes fastest.
Arguments:
- background: float32 [3, 65536], P(None, ('groups', 'dom', 'sub')), parts along dimension 1, may hold values from -6 to 6
- obs_weight: float32 [65536], P(('groups', 'dom', 'sub')), parts along dimension 0, may hold values from 0.02 to 0.2
- connect: int32 [10, 32768], P(None, ('groups', 'dom', 'sub', 'field')), parts along dimension 1, may hold values from 0 to 5631, as said below
- live_blocks: int32 [32], P(('groups', 'dom', 'sub', 'field')), parts along dimension 0, may hold values from 2 to 8, as said below
- elem_scale: float32 [32768], P(('groups', 'dom', 'sub', 'field')), parts along dimension 0, may hold values from 0.5 to 2
- reg_weight: float32 [32768], P(('groups', 'dom', 'sub', 'field')), parts along dimension 0, may hold values from 0.2 to 2
- iterate: float32 [32768], P(('groups', 'dom', 'sub', 'field')), parts along dimension 0, may hold values from -6 to 6
- residual: float32 [32768], P(('groups', 'dom', 'sub', 'field')), parts along dimension 0, may hold values from -30 to 30
- direction: float32 [32768], P(('groups', 'dom', 'sub', 'field')), parts along dimension 0, may hold values from -30 to 30
- send_nodes: int32 [16, 3, 2, 256], P(('groups', 'dom', 'sub')), parts along dimension 0, may hold values from 0 to 4095, as said below
- send_count: int32 [16, 3, 2], P(('groups', 'dom', 'sub')), parts along dimension 0, may hold values from 0 to 256, as said below
- ref_stiff: float32 [30, 30], replicated, may hold values from -1.05 to 4.05, as said below
Outputs:
- iterate_next: float32 [32768], P(('groups', 'dom', 'sub', 'field')), parts along dimension 0
- residual_next: float32 [32768], P(('groups', 'dom', 'sub', 'field')), parts along dimension 0
- direction_next: float32 [32768], P(('groups', 'dom', 'sub', 'field')), parts along dimension 0
There are 2 independent parts, one for each index of `groups`. A program takes and returns all parts, laid end to end along the dimension named above; an argument that names none is the same for every part. Nothing has to cross between parts.
Inputs may be any that keep to these rules, and one draw needn't show every extreme that they name: `send_nodes`: for every link the first send_count slots hold distinct owned nodes; later slots are padding. `send_count`: links go only to partitions of dom index d - 1, d or d + 1 and never to the sender itself or past the ends of dom; some link is full with 256 slots. `connect`: entries from 4096 on name ghost slots that are live slots of their owner's link. `live_blocks`: live blocks fill a device's slots from its first one; some device has 8. `ref_stiff`: Symmetric.
All inputs are finite; a program needn't handle non-finite values.
Results may differ from a plain program's by a relative error of at most 0.00005.
Values sent between devices are 32-bit elements; how exact they have to be, the bound alone decides.
A program may use at most 64 MiB of HBM per device.

v0:
```python
import jax
import jax.numpy as jnp
from jax import lax
from jax.sharding import PartitionSpec as P

BLK = 128


def extended(cells, sides, width):
    for axis, dim in sides:
        count = lax.axis_size(axis)
        ends = count - 1
        head = lax.slice_in_dim(cells, 0, width, axis=dim)
        tail = lax.slice_in_dim(cells, cells.shape[dim] - width, cells.shape[dim], axis=dim)
        cells = jnp.concatenate(
            [
                lax.ppermute(tail, axis, [(i, (i + 1) % count) for i in range(ends)]),
                cells,
                lax.ppermute(head, axis, [((i + 1) % count, i) for i in range(ends)]),
            ],
            axis=dim,
        )
    return cells


def on_device(
    background,
    obs_weight,
    connect,
    live_blocks,
    elem_scale,
    reg_weight,
    iterate,
    residual,
    direction,
    send_nodes,
    send_count,
    ref_stiff,
):
    owned_nodes = background.shape[1]
    sub_count = lax.axis_size("sub")
    link_slots = send_nodes.shape[3]
    element_count = connect.shape[1]
    ghost_slots = 3 * sub_count * link_slots
    targets = send_nodes[0].reshape(-1)
    open_slot = (
        jnp.arange(link_slots, dtype=jnp.int32)[None, None, :] < send_count[0][:, :, None]
    ).astype(jnp.float32)

    def fetch_ghosts(values):
        outbound = values[:, targets].reshape(3, 3, sub_count, link_slots) * open_slot[None]
        mixed = lax.all_to_all(outbound, "sub", split_axis=2, concat_axis=2, tiled=True)
        rimmed = extended(mixed, (("dom", 1),), 1)
        arrived = rimmed[:, 0::2]
        return jnp.concatenate([values, arrived.reshape(3, ghost_slots)], axis=1)

    element = jnp.arange(element_count, dtype=jnp.int32)
    live_mask = (element < BLK * live_blocks[0]).astype(jnp.float32)
    search = live_mask * direction
    remain = live_mask * residual
    guess = live_mask * iterate
    flat_connect = connect.reshape(-1)
    state_full = fetch_ghosts(background)
    element_state = state_full[:, connect].reshape(30, element_count)
    coupled = (live_mask * elem_scale)[None, :] * jnp.dot(
        ref_stiff, element_state, precision=lax.Precision.HIGHEST
    )
    terms = (search[None, :] * coupled).reshape(3, -1)
    accumulated = (
        jnp.zeros((3, owned_nodes + ghost_slots), jnp.float32).at[:, flat_connect].add(terms)
    )
    accumulated = lax.psum(accumulated, "field")
    returning = accumulated[:, owned_nodes:].reshape(3, 3, sub_count, link_slots)
    rimmed = extended(returning, (("dom", 1),), 1)
    landed = lax.all_to_all(rimmed[:, 0::2], "sub", split_axis=2, concat_axis=2, tiled=True)
    landed = (landed * open_slot[None]).reshape(3, -1)
    assembled = accumulated[:, :owned_nodes] + jnp.zeros((3, owned_nodes), jnp.float32).at[
        :, targets
    ].add(landed)
    weighted = obs_weight[None, :] * assembled
    weighted_full = fetch_ghosts(weighted)
    pulled = weighted_full[:, connect].reshape(30, element_count)
    hess_search = jnp.sum(coupled * pulled, axis=0) + reg_weight * search
    squared_before, curvature_sum, cross_term, image_square = lax.psum(
        (
            jnp.sum(remain * remain),
            jnp.sum(search * hess_search),
            jnp.sum(remain * hess_search),
            jnp.sum(hess_search * hess_search),
        ),
        ("dom", "sub", "field"),
    )
    step_length = squared_before / curvature_sum
    iterate_next = guess + step_length * search
    residual_next = remain - step_length * hess_search
    squared_after = (
        squared_before - 2.0 * step_length * cross_term + step_length * step_length * image_square
    )
    direction_next = residual_next + squared_after / squared_before * search
    return (iterate_next, residual_next, direction_next)


def solution(mesh):
    placed = (
        P(None, ("groups", "dom", "sub")),
        P(("groups", "dom", "sub")),
        P(None, ("groups", "dom", "sub", "field")),
        P(("groups", "dom", "sub", "field")),
        P(("groups", "dom", "sub", "field")),
        P(("groups", "dom", "sub", "field")),
        P(("groups", "dom", "sub", "field")),
        P(("groups", "dom", "sub", "field")),
        P(("groups", "dom", "sub", "field")),
        P(("groups", "dom", "sub"), None, None, None),
        P(("groups", "dom", "sub"), None, None),
        P(),
    )
    return jax.shard_map(
        on_device,
        mesh=mesh,
        in_specs=placed,
        out_specs=(
            P(("groups", "dom", "sub", "field")),
            P(("groups", "dom", "sub", "field")),
            P(("groups", "dom", "sub", "field")),
        ),
        check_vma=False,
    )
```

profile of v0, /device:TPU:0, one launch (start us, length us, event | category | flops | bytes accessed | tf_op | source)
XLA Modules:
  0.0 283.6 jit_solution(14023031561616133790)
XLA Ops:
  7.2 0.0 copy-start
  7.2 0.0 copy-start.2
  7.2 0.0 copy-start.3
  7.2 0.0 copy-start.7
  7.2 0.0 copy-start.6
  7.2 0.8 reshape_squeeze.3
  8.0 0.8 fusion.4
  8.8 1.5 copy.66
  10.3 2.6 gather_fusion
  12.9 0.3 copy.67
  13.2 0.6 broadcast_multiply_fusion.4
  13.8 4.2 %all-to-all-start = ((f32[3,3,2,256]{3,1,0,2:T(4,128)}), f32[3,3,2,256]{3,1,0,2:T(4,128)S(1)}, u32[]{:S(2)}, u32[]{:S(2)}) async-start(f32[3,3,2,256]{3,1,0,2:T(4,128)} %broadcast_multiply_fusion.4), calls=%async_computation | async-start | bytes 49152 | tf_op jit(solution)/shard_map/all_to_all | solution.py:52
  18.1 0.0 all-reduce.3.cloned.1.call-start
  18.1 0.0 copy-done.3
  18.9 3.1 %all-to-all-done = f32[3,3,2,256]{3,1,0,2:T(4,128)S(1)} async-done(((f32[3,3,2,256]{3,1,0,2:T(4,128)}), f32[3,3,2,256]{3,1,0,2:T(4,128)S(1)}, u32[]{:S(2)}, u32[]{:S(2)}) %all-to-all-start) | async-done | bytes 18464 | tf_op jit(solution)/shard_map/all_to_all | solution.py:52
  22.0 4.0 %collective-permute-start = (f32[3,1,2,256]{3,1,0,2:T(1,128)S(1)}, f32[3,1,2,256]{3,1,0,2:T(1,128)S(1)}, u32[]{:S(2)}, u32[]{:S(2)}) collective-permute-start(f32[3,1,2,256]{3,1,0,2:T(1,128)S(1)} %get-tuple-element.18), channel_id=1, source_target_pairs={{0,4},{4,8},{8,12},{1,5},{5,9},{9,13},{2,6},{6,10},{10,14},{3,7},{... | collective-permute-start | bytes 18440 | tf_op jit(solution)/shard_map/ppermute | solution.py:17
  25.9 1.3 collective-permute-start.1
  27.2 0.0 copy-done.7
  27.3 0.0 copy-done.6
  27.3 0.0 collective-permute-done
  27.3 4.1 %collective-permute-done.1 = f32[3,1,2,256]{3,1,0,2:T(1,128)S(1)} collective-permute-done((f32[3,1,2,256]{3,1,0,2:T(1,128)S(1)}, f32[3,1,2,256]{3,1,0,2:T(1,128)S(1)}, u32[]{:S(2)}, u32[]{:S(2)}) %collective-permute-start.1) | collective-permute-done | bytes 6176 | tf_op jit(solution)/shard_map/ppermute | solution.py:19
  31.5 0.0 copy-done.2
  31.6 0.8 copy.71
  32.4 34.2 %gather_fusion.1 = f32[10240,3]{1,0:T(8,128)} fusion(f32[3,5632]{0,1:T(8,128)S(1)} %copy.71, s32[10240]{0:T(1024)S(1)} %broadcast_clamp_fusion), kind=kCustom, calls=%fused_computation.1 | custom fusion | bytes 286720 | tf_op jit(solution)/shard_map/gather | solution.py:64
  66.7 4.2 %copy.72 = f32[10,1024,3]{1,0,2:T(8,128)S(1)} copy(f32[10,1024,3]{2,1,0:T(8,128)} %bitcast.28) | data formatting | bytes 245760 | tf_op jit(solution)/shard_map/gather | solution.py:64
  70.9 0.0 copy-done
  70.9 0.3 broadcast_multiply_fusion.1
  71.2 0.1 reshape.145
  71.3 3.1 %copy.73 = f32[3,10240]{0,1:T(8,128)} copy(f32[3,10240]{1,0:T(4,128)S(1)} %reshape.145) | data formatting | bytes 245760 | tf_op jit(solution)/shard_map/reshape | solution.py:68
  74.4 51.9 %scatter_custom_fusion = f32[3,5632]{0,1:T(8,128)} fusion(s32[10240]{0:T(1024)S(1)} %bitcast.38, f32[3,10240]{0,1:T(8,128)} %copy.73, f32[]{:T(128)} %constant.7.clone.1), kind=kCustom, calls=%fused_computation.6 | custom fusion | flops 30720 | bytes 190468 | tf_op jit(solution)/shard_map/scatter-add | solution.py:70
  126.3 0.0 all-reduce.3.cloned.1.call-update
  126.3 22.3 %all-reduce.3.cloned.1.call-done = f32[3,5632]{0,1:T(8,128)} async-done(((f32[3,5632]{0,1:T(8,128)}), f32[3,5632]{0,1:T(8,128)}) %all-reduce.3.cloned.1.call-update) | async-done | bytes 67600 | tf_op jit(solution)/shard_map/psum | solution.py:72
  148.6 1.2 slice.55
  149.7 0.3 copy.74
  150.1 0.0 copy-start.4
  150.1 3.8 %collective-permute-start.2 = (f32[3,1,2,256]{3,1,0,2:T(1,128)S(1)}, f32[3,1,2,256]{3,1,0,2:T(1,128)S(1)}, u32[]{:S(2)}, u32[]{:S(2)}) collective-permute-start(f32[3,1,2,256]{3,1,0,2:T(1,128)S(1)} %get-tuple-element.16), channel_id=1, source_target_pairs={{0,4},{4,8},{8,12},{1,5},{5,9},{9,13},{2,6},{6,10},{10,14},{3,7},{... | collective-permute-start | bytes 18440 | tf_op jit(solution)/shard_map/ppermute | solution.py:17
  153.9 1.3 collective-permute-start.3
  155.2 0.0 collective-permute-done.2
  155.2 4.2 %collective-permute-done.3 = f32[3,1,2,256]{3,1,0,2:T(1,128)S(1)} collective-permute-done((f32[3,1,2,256]{3,1,0,2:T(1,128)S(1)}, f32[3,1,2,256]{3,1,0,2:T(1,128)S(1)}, u32[]{:S(2)}, u32[]{:S(2)}) %collective-permute-start.3) | collective-permute-done | bytes 6176 | tf_op jit(solution)/shard_map/ppermute | solution.py:19
  159.5 0.7 slice.40
  160.1 3.2 %all-to-all-start.1 = ((f32[3,3,2,256]{3,1,0,2:T(4,128)}), f32[3,3,2,256]{3,1,0,2:T(4,128)S(1)}, u32[]{:S(2)}, u32[]{:S(2)}) async-start(f32[3,3,2,256]{3,1,0,2:T(4,128)} %slice.40), calls=%async_computation.1 | async-start | bytes 49152 | tf_op jit(solution)/shard_map/all_to_all | solution.py:75
  163.4 3.9 %all-to-all-done.1 = f32[3,3,2,256]{3,1,0,2:T(4,128)S(1)} async-done(((f32[3,3,2,256]{3,1,0,2:T(4,128)}), f32[3,3,2,256]{3,1,0,2:T(4,128)S(1)}, u32[]{:S(2)}, u32[]{:S(2)}) %all-to-all-start.1) | async-done | bytes 18464 | tf_op jit(solution)/shard_map/all_to_all | solution.py:75
  167.3 0.3 copy.78
  167.6 0.0 slice-done
  167.6 9.5 %scatter_fusion = f32[3,4096]{0,1:T(8,128)S(1)} fusion(f32[3,4096]{0,1:T(8,128)S(1)} %slice-done, s32[1536]{0:T(1024)S(1)} %fusion.5, f32[1536,3]{1,0:T(8,128)S(1)} %copy.78), kind=kCustom, calls=%fused_computation.5 | custom fusion | flops 4608 | bytes 61440 | tf_op jit(solution)/shard_map/scatter-add | solution.py:79
  177.1 0.0 copy-done.4
  177.2 1.9 broadcast_multiply_fusion
  179.1 4.3 %gather_fusion.2 = f32[1536,3]{1,0:T(8,128)S(1)} fusion(f32[3,4096]{0,1:T(8,128)} %broadcast_multiply_fusion, s32[2048]{0:T(1024)S(1)} %pad_clamp_fusion), kind=kCustom, calls=%fused_computation.2 | custom fusion | bytes 43008 | tf_op jit(solution)/shard_map/gather | solution.py:51
  183.4 0.3 copy.79
  183.8 6.3 %all_to_all.15 = f32[3,3,2,256]{3,1,0,2:T(4,128)S(1)} all-to-all(f32[3,3,2,256]{3,1,0,2:T(4,128)S(1)} %broadcast_multiply_fusion.2), channel_id=1, replica_groups=mesh['groups'=2,'dom'=4,'sub'=2,'field'=2] {'sub'}, dimensions={2} | all-to-all | bytes 36864 | tf_op jit(solution)/shard_map/all_to_all | solution.py:52
  190.1 3.4 %collective-permute-start.4 = (f32[3,1,2,256]{3,1,0,2:T(1,128)S(1)}, f32[3,1,2,256]{3,1,0,2:T(1,128)S(1)}, u32[]{:S(2)}, u32[]{:S(2)}) collective-permute-start(f32[3,1,2,256]{3,1,0,2:T(1,128)S(1)} %get-tuple-element.14), channel_id=1, source_target_pairs={{0,4},{4,8},{8,12},{1,5},{5,9},{9,13},{2,6},{6,10},{10,14},{3,7},{... | collective-permute-start | bytes 18440 | tf_op jit(solution)/shard_map/ppermute | solution.py:17
  193.5 1.3 collective-permute-start.5
  194.8 0.0 collective-permute-done.4
  194.8 4.2 %collective-permute-done.5 = f32[3,1,2,256]{3,1,0,2:T(1,128)S(1)} collective-permute-done((f32[3,1,2,256]{3,1,0,2:T(1,128)S(1)}, f32[3,1,2,256]{3,1,0,2:T(1,128)S(1)}, u32[]{:S(2)}, u32[]{:S(2)}) %collective-permute-start.5) | collective-permute-done | bytes 6176 | tf_op jit(solution)/shard_map/ppermute | solution.py:19
  199.0 0.3 copy.83
  199.3 0.0 copy-done.1
  199.3 1.7 pad_maximum_fusion
  201.1 36.1 %gather_fusion.3 = f32[10240,3]{1,0:T(8,128)} fusion(f32[3,5632]{0,1:T(8,128)} %pad_maximum_fusion, s32[10240]{0:T(1024)S(1)} %broadcast_clamp_fusion), kind=kCustom, calls=%fused_computation.3 | custom fusion | bytes 286720 | tf_op jit(solution)/shard_map/gather | solution.py:82
  237.1 4.2 %copy.84 = f32[10,1024,3]{1,0,2:T(8,128)S(1)} copy(f32[10,1024,3]{2,1,0:T(8,128)} %bitcast.27) | data formatting | bytes 245760 | tf_op jit(solution)/shard_map/gather | solution.py:82
  241.4 0.0 copy-done.5
  241.4 0.6 multiply_reduce_fusion.1
  242.1 30.1 %all-reduce = (f32[]{:T(128)}, f32[]{:T(128)}, f32[]{:T(128)}, f32[]{:T(128)}) all-reduce(f32[]{:T(128)} %get-tuple-element.5, f32[]{:T(128)} %get-tuple-element.6, f32[]{:T(128)} %get-tuple-element.4, f32[]{:T(128)} %get-tuple-element.3), channel_id=1, replica_groups=mesh['groups'=2,'dom'=4,'sub'=2,'field'=2] {'dom','sub','field'}, use_global_device_ids=true, to_apply=%region_1.0 | all-reduce | flops 4 | bytes 32 | tf_op jit(solution)/shard_map/psum | solution.py:84
  276.1 0.0 copy-done.9
  276.2 0.6 multiply_add_fusion
  (37 shorter events, 0.5 us)
Async XLA Ops:
  7.2 63.7 %copy-start = (f32[30,30]{1,0:T(8,128)S(1)}, f32[30,30]{1,0:T(8,128)}, u32[]{:S(2)}) copy-start(f32[30,30]{1,0:T(8,128)} %param.23) | copy-start | bytes 10804
  7.2 24.4 %copy-start.2 = (f32[3,4096]{1,0:T(4,128)S(1)}, f32[3,4096]{1,0:T(4,128)}, u32[]{:S(2)}) copy-start(f32[3,4096]{1,0:T(4,128)} %param.12) | copy-start | bytes 147460
  7.2 10.9 %copy-start.3 = (s32[10,1024]{1,0:T(8,128)S(1)}, s32[10,1024]{1,0:T(8,128)}, u32[]{:S(2)}) copy-start(s32[10,1024]{1,0:T(8,128)} %param.14) | copy-start | bytes 122884
  7.2 20.0 %copy-start.7 = (f32[1024]{0:T(1024)S(1)}, f32[1024]{0:T(1024)}, u32[]{:S(2)}) copy-start(f32[1024]{0:T(1024)} %param.20) | copy-start | bytes 12292
  7.2 20.0 %copy-start.6 = (f32[1024]{0:T(1024)S(1)}, f32[1024]{0:T(1024)}, u32[]{:S(2)}) copy-start(f32[1024]{0:T(1024)} %param.16) | copy-start | bytes 12292
  13.8 8.1 %all-to-all-start = ((f32[3,3,2,256]{3,1,0,2:T(4,128)}), f32[3,3,2,256]{3,1,0,2:T(4,128)S(1)}, u32[]{:S(2)}, u32[]{:S(2)}) async-start(f32[3,3,2,256]{3,1,0,2:T(4,128)} %broadcast_multiply_fusion.4), calls=%async_computation | async-start | bytes 49152 | tf_op jit(solution)/shard_map/all_to_all | solution.py:52
  18.1 130.5 %all-reduce.3.cloned.1.call-start = ((), (), s32[]{:S(2)}) async-start(), calls=%async_computation.3 | async-start | bytes 5767168 | tf_op jit(solution)/shard_map/psum | solution.py:72
  22.0 5.3 %collective-permute-start = (f32[3,1,2,256]{3,1,0,2:T(1,128)S(1)}, f32[3,1,2,256]{3,1,0,2:T(1,128)S(1)}, u32[]{:S(2)}, u32[]{:S(2)}) collective-permute-start(f32[3,1,2,256]{3,1,0,2:T(1,128)S(1)} %get-tuple-element.18), channel_id=1, source_target_pairs={{0,4},{4,8},{8,12},{1,5},{5,9},{9,13},{2,6},{6,10},{10,14},{3,7},{... | collective-permute-start | bytes 18440 | tf_op jit(solution)/shard_map/ppermute | solution.py:17
  25.9 5.5 %collective-permute-start.1 = (f32[3,1,2,256]{3,1,0,2:T(1,128)S(1)}, f32[3,1,2,256]{3,1,0,2:T(1,128)S(1)}, u32[]{:S(2)}, u32[]{:S(2)}) collective-permute-start(f32[3,1,2,256]{3,1,0,2:T(1,128)S(1)} %get-tuple-element.19), channel_id=1, source_target_pairs={{4,0},{8,4},{12,8},{5,1},{9,5},{13,9},{6,2},{10,6},{14,10},{7,3},{... | collective-permute-start | bytes 18440 | tf_op jit(solution)/shard_map/ppermute | solution.py:19
  150.1 17.5 %slice-start = ((f32[3,5632]{0,1:T(8,128)}), f32[3,4096]{0,1:T(8,128)S(1)}, s32[]{:S(2)}) async-start(f32[3,5632]{0,1:T(8,128)} %all-reduce.3.cloned.1.call-done), calls=%async_computation.4 | async-start | bytes 4194304 | tf_op jit(solution)/shard_map/slice | solution.py:77
  150.1 27.0 %copy-start.4 = (f32[4096]{0:T(1024)S(1)}, f32[4096]{0:T(1024)}, u32[]{:S(2)}) copy-start(f32[4096]{0:T(1024)} %param.13) | copy-start | bytes 49156
  150.1 5.1 %collective-permute-start.2 = (f32[3,1,2,256]{3,1,0,2:T(1,128)S(1)}, f32[3,1,2,256]{3,1,0,2:T(1,128)S(1)}, u32[]{:S(2)}, u32[]{:S(2)}) collective-permute-start(f32[3,1,2,256]{3,1,0,2:T(1,128)S(1)} %get-tuple-element.16), channel_id=1, source_target_pairs={{0,4},{4,8},{8,12},{1,5},{5,9},{9,13},{2,6},{6,10},{10,14},{3,7},{... | collective-permute-start | bytes 18440 | tf_op jit(solution)/shard_map/ppermute | solution.py:17
  153.9 5.5 %collective-permute-start.3 = (f32[3,1,2,256]{3,1,0,2:T(1,128)S(1)}, f32[3,1,2,256]{3,1,0,2:T(1,128)S(1)}, u32[]{:S(2)}, u32[]{:S(2)}) collective-permute-start(f32[3,1,2,256]{3,1,0,2:T(1,128)S(1)} %get-tuple-element.17), channel_id=1, source_target_pairs={{4,0},{8,4},{12,8},{5,1},{9,5},{13,9},{6,2},{10,6},{14,10},{7,3},{... | collective-permute-start | bytes 18440 | tf_op jit(solution)/shard_map/ppermute | solution.py:19
  160.1 7.1 %all-to-all-start.1 = ((f32[3,3,2,256]{3,1,0,2:T(4,128)}), f32[3,3,2,256]{3,1,0,2:T(4,128)S(1)}, u32[]{:S(2)}, u32[]{:S(2)}) async-start(f32[3,3,2,256]{3,1,0,2:T(4,128)} %slice.40), calls=%async_computation.1 | async-start | bytes 49152 | tf_op jit(solution)/shard_map/all_to_all | solution.py:75
  179.1 20.2 %copy-start.1 = (f32[3,4096]{0,1:T(8,128)S(1)}, f32[3,4096]{0,1:T(8,128)}, u32[]{:S(2)}) copy-start(f32[3,4096]{0,1:T(8,128)} %broadcast_multiply_fusion) | copy-start | bytes 147460
  190.1 4.7 %collective-permute-start.4 = (f32[3,1,2,256]{3,1,0,2:T(1,128)S(1)}, f32[3,1,2,256]{3,1,0,2:T(1,128)S(1)}, u32[]{:S(2)}, u32[]{:S(2)}) collective-permute-start(f32[3,1,2,256]{3,1,0,2:T(1,128)S(1)} %get-tuple-element.14), channel_id=1, source_target_pairs={{0,4},{4,8},{8,12},{1,5},{5,9},{9,13},{2,6},{6,10},{10,14},{3,7},{... | collective-permute-start | bytes 18440 | tf_op jit(solution)/shard_map/ppermute | solution.py:17
  193.5 5.5 %collective-permute-start.5 = (f32[3,1,2,256]{3,1,0,2:T(1,128)S(1)}, f32[3,1,2,256]{3,1,0,2:T(1,128)S(1)}, u32[]{:S(2)}, u32[]{:S(2)}) collective-permute-start(f32[3,1,2,256]{3,1,0,2:T(1,128)S(1)} %get-tuple-element.15), channel_id=1, source_target_pairs={{4,0},{8,4},{12,8},{5,1},{9,5},{13,9},{6,2},{10,6},{14,10},{7,3},{... | collective-permute-start | bytes 18440 | tf_op jit(solution)/shard_map/ppermute | solution.py:19
  237.1 4.3 %copy-start.5 = (f32[1024]{0:T(1024)S(1)}, f32[1024]{0:T(1024)}, u32[]{:S(2)}) copy-start(f32[1024]{0:T(1024)} %param.19) | copy-start | bytes 12292
  237.1 4.3 %copy-start.8 = (f32[1024]{0:T(1024)S(1)}, f32[1024]{0:T(1024)}, u32[]{:S(2)}) copy-start(f32[1024]{0:T(1024)} %param.17) | copy-start | bytes 12292
  237.1 39.0 %copy-start.9 = (f32[1024]{0:T(1024)S(1)}, f32[1024]{0:T(1024)}, u32[]{:S(2)}) copy-start(f32[1024]{0:T(1024)} %param.18) | copy-start | bytes 12292
Sparse Core Ops, SparseCore 0:
  126.4 22.0 all-reduce.2
where the time goes:
time: 284 us
  local copies, waits for them, and re-layouts  95.7 us (34%)
  other arithmetic  67.9 us (24%)
  waiting for transfers between devices  41.8 us (15%)
  blocking collectives  36.4 us (13%)
  starting transfers between devices  22.5 us (8%)
  between operations  19.1 us (7%)
    scatter-add x1, other arithmetic, on_device(): jnp.zeros((3, owned_nodes + ghost_slots), jnp.float32).at[:, flat_connect]  51.9 us
    gather x2, local copies, waits for them, and re-layouts, on_device(): pulled = weighted_full[:, connect].reshape(30, element_count)  40.3 us
    gather x2, local copies, waits for them, and re-layouts, on_device(): element_state = state_full[:, connect].reshape(30, element_count)  38.4 us
    psum x1, blocking collectives, on_device(): lax.psum((jnp.sum(remain * remain), jnp.sum(search * hess_search), jnp.su...  30.1 us
    psum x1, waiting for transfers between devices, on_device(): accumulated = lax.psum(accumulated, 'field')  22.3 us
    ppermute x3, waiting for transfers between devices, extended(): lax.ppermute(head, axis, [((i + 1) % count, i) for i in range(ends)])  12.5 us
    ppermute x3, starting transfers between devices, extended(): lax.ppermute(tail, axis, [(i, (i + 1) % count) for i in range(ends)])  11.1 us
    scatter-add x1, other arithmetic, on_device(): assembled = accumulated[:, :owned_nodes] + jnp.zeros((3, owned_nodes), jn...  9.52 us
  transfers between devices with their start and end apart: 9, of which 6 were waited for; matrix products, arithmetic and copies ran while one was open for 0% of the time, Pallas kernels for 0%

commit v1 on v0

--- a/solution.py
+++ b/solution.py
@@ -82,13 +82,16 @@
     pulled = weighted_full[:, connect].reshape(30, element_count)
     hess_search = jnp.sum(coupled * pulled, axis=0) + reg_weight * search
     squared_before, curvature_sum, cross_term, image_square = lax.psum(
-        (
-            jnp.sum(remain * remain),
-            jnp.sum(search * hess_search),
-            jnp.sum(remain * hess_search),
-            jnp.sum(hess_search * hess_search),
+        lax.psum(
+            (
+                jnp.sum(remain * remain),
+                jnp.sum(search * hess_search),
+                jnp.sum(remain * hess_search),
+                jnp.sum(hess_search * hess_search),
+            ),
+            ("sub", "field"),
         ),
-        ("dom", "sub", "field"),
+        "dom",
     )
     step_length = squared_before / curvature_sum
     iterate_next = guess + step_length * search

time: 284 us -> 271 us (0.954)
  blocking collectives: 36.4 us -> 23.2 us
    psum x1, blocking collectives: 30.1 us -> 6.39 us  [on_device(): lax.psum((jnp.sum(remain * remain), jnp.sum(search * hess_search), jnp.su...]
    psum x0 -> x1, blocking collectives: none -> 10.5 us  [on_device(): lax.psum(lax.psum((jnp.sum(remain * remain), jnp.sum(search * hess_search...]
where the time goes in v1:
time: 271 us
  local copies, waits for them, and re-layouts  95.7 us (35%)
  other arithmetic  68 us (25%)
  waiting for transfers between devices  41.8 us (15%)
  blocking collectives  23.2 us (9%)
  starting transfers between devices  22.5 us (8%)
  between operations  19.1 us (7%)
    scatter-add x1, other arithmetic, on_device(): jnp.zeros((3, owned_nodes + ghost_slots), jnp.float32).at[:, flat_connect]  51.9 us
    gather x2, local copies, waits for them, and re-layouts, on_device(): pulled = weighted_full[:, connect].reshape(30, element_count)  40.3 us
    gather x2, local copies, waits for them, and re-layouts, on_device(): element_state = state_full[:, connect].reshape(30, element_count)  38.5 us
    psum x1, waiting for transfers between devices, on_device(): accumulated = lax.psum(accumulated, 'field')  22.3 us
    ppermute x3, waiting for transfers between devices, extended(): lax.ppermute(head, axis, [((i + 1) % count, i) for i in range(ends)])  12.5 us
    ppermute x3, starting transfers between devices, extended(): lax.ppermute(tail, axis, [(i, (i + 1) % count) for i in range(ends)])  11.1 us
    psum x1, blocking collectives, on_device(): lax.psum(lax.psum((jnp.sum(remain * remain), jnp.sum(search * hess_search...  10.5 us
    scatter-add x1, other arithmetic, on_device(): assembled = accumulated[:, :owned_nodes] + jnp.zeros((3, owned_nodes), jn...  9.52 us
  transfers between devices with their start and end apart: 9, of which 6 were waited for; matrix products, arithmetic and copies ran while one was open for 0% of the time, Pallas kernels for 0%

profile of v1, /device:TPU:0, one launch (start us, length us, event | category | flops | bytes accessed | tf_op | source)
XLA Modules:
  0.0 270.5 jit_solution(7915630861587051021)
XLA Ops:
  7.2 0.0 copy-start
  7.2 0.0 copy-start.2
  7.2 0.0 copy-start.3
  7.2 0.0 copy-start.7
  7.2 0.0 copy-start.6
  7.2 0.8 reshape_squeeze.3
  8.0 0.8 fusion.4
  8.8 1.5 copy.66
  10.3 2.6 gather_fusion
  12.9 0.3 copy.67
  13.2 0.6 broadcast_multiply_fusion.4
  13.8 4.2 %all-to-all-start = ((f32[3,3,2,256]{3,1,0,2:T(4,128)}), f32[3,3,2,256]{3,1,0,2:T(4,128)S(1)}, u32[]{:S(2)}, u32[]{:S(2)}) async-start(f32[3,3,2,256]{3,1,0,2:T(4,128)} %broadcast_multiply_fusion.4), calls=%async_computation | async-start | bytes 49152 | tf_op jit(solution)/shard_map/all_to_all | solution.py:52
  18.1 0.0 all-reduce.4.cloned.1.call-start
  18.1 0.0 copy-done.3
  18.9 3.1 %all-to-all-done = f32[3,3,2,256]{3,1,0,2:T(4,128)S(1)} async-done(((f32[3,3,2,256]{3,1,0,2:T(4,128)}), f32[3,3,2,256]{3,1,0,2:T(4,128)S(1)}, u32[]{:S(2)}, u32[]{:S(2)}) %all-to-all-start) | async-done | bytes 18464 | tf_op jit(solution)/shard_map/all_to_all | solution.py:52
  22.0 4.0 %collective-permute-start = (f32[3,1,2,256]{3,1,0,2:T(1,128)S(1)}, f32[3,1,2,256]{3,1,0,2:T(1,128)S(1)}, u32[]{:S(2)}, u32[]{:S(2)}) collective-permute-start(f32[3,1,2,256]{3,1,0,2:T(1,128)S(1)} %get-tuple-element.22), channel_id=1, source_target_pairs={{0,4},{4,8},{8,12},{1,5},{5,9},{9,13},{2,6},{6,10},{10,14},{3,7},{... | collective-permute-start | bytes 18440 | tf_op jit(solution)/shard_map/ppermute | solution.py:17
  25.9 1.3 collective-permute-start.1
  27.2 0.0 copy-done.7
  27.3 0.0 copy-done.6
  27.3 0.0 collective-permute-done
  27.3 4.1 %collective-permute-done.1 = f32[3,1,2,256]{3,1,0,2:T(1,128)S(1)} collective-permute-done((f32[3,1,2,256]{3,1,0,2:T(1,128)S(1)}, f32[3,1,2,256]{3,1,0,2:T(1,128)S(1)}, u32[]{:S(2)}, u32[]{:S(2)}) %collective-permute-start.1) | collective-permute-done | bytes 6176 | tf_op jit(solution)/shard_map/ppermute | solution.py:19
  31.5 0.0 copy-done.2
  31.6 0.8 copy.71
  32.4 34.3 %gather_fusion.1 = f32[10240,3]{1,0:T(8,128)} fusion(f32[3,5632]{0,1:T(8,128)S(1)} %copy.71, s32[10240]{0:T(1024)S(1)} %broadcast_clamp_fusion), kind=kCustom, calls=%fused_computation.1 | custom fusion | bytes 286720 | tf_op jit(solution)/shard_map/gather | solution.py:64
  66.7 4.2 %copy.72 = f32[10,1024,3]{1,0,2:T(8,128)S(1)} copy(f32[10,1024,3]{2,1,0:T(8,128)} %bitcast.28) | data formatting | bytes 245760 | tf_op jit(solution)/shard_map/gather | solution.py:64
  70.9 0.0 copy-done
  70.9 0.3 broadcast_multiply_fusion.1
  71.2 0.1 reshape.145
  71.3 3.1 %copy.73 = f32[3,10240]{0,1:T(8,128)} copy(f32[3,10240]{1,0:T(4,128)S(1)} %reshape.145) | data formatting | bytes 245760 | tf_op jit(solution)/shard_map/reshape | solution.py:68
  74.4 51.9 %scatter_custom_fusion = f32[3,5632]{0,1:T(8,128)} fusion(s32[10240]{0:T(1024)S(1)} %bitcast.38, f32[3,10240]{0,1:T(8,128)} %copy.73, f32[]{:T(128)} %constant.7.clone.1), kind=kCustom, calls=%fused_computation.6 | custom fusion | flops 30720 | bytes 190468 | tf_op jit(solution)/shard_map/scatter-add | solution.py:70
  126.3 0.0 all-reduce.4.cloned.1.call-update
  126.3 22.3 %all-reduce.4.cloned.1.call-done = f32[3,5632]{0,1:T(8,128)} async-done(((f32[3,5632]{0,1:T(8,128)}), f32[3,5632]{0,1:T(8,128)}) %all-reduce.4.cloned.1.call-update) | async-done | bytes 67600 | tf_op jit(solution)/shard_map/psum | solution.py:72
  148.6 1.2 slice.55
  149.8 0.3 copy.74
  150.1 0.0 copy-start.4
  150.1 3.8 %collective-permute-start.2 = (f32[3,1,2,256]{3,1,0,2:T(1,128)S(1)}, f32[3,1,2,256]{3,1,0,2:T(1,128)S(1)}, u32[]{:S(2)}, u32[]{:S(2)}) collective-permute-start(f32[3,1,2,256]{3,1,0,2:T(1,128)S(1)} %get-tuple-element.20), channel_id=1, source_target_pairs={{0,4},{4,8},{8,12},{1,5},{5,9},{9,13},{2,6},{6,10},{10,14},{3,7},{... | collective-permute-start | bytes 18440 | tf_op jit(solution)/shard_map/ppermute | solution.py:17
  153.9 1.3 collective-permute-start.3
  155.2 0.0 collective-permute-done.2
  155.3 4.2 %collective-permute-done.3 = f32[3,1,2,256]{3,1,0,2:T(1,128)S(1)} collective-permute-done((f32[3,1,2,256]{3,1,0,2:T(1,128)S(1)}, f32[3,1,2,256]{3,1,0,2:T(1,128)S(1)}, u32[]{:S(2)}, u32[]{:S(2)}) %collective-permute-start.3) | collective-permute-done | bytes 6176 | tf_op jit(solution)/shard_map/ppermute | solution.py:19
  159.5 0.7 slice.40
  160.1 3.2 %all-to-all-start.1 = ((f32[3,3,2,256]{3,1,0,2:T(4,128)}), f32[3,3,2,256]{3,1,0,2:T(4,128)S(1)}, u32[]{:S(2)}, u32[]{:S(2)}) async-start(f32[3,3,2,256]{3,1,0,2:T(4,128)} %slice.40), calls=%async_computation.1 | async-start | bytes 49152 | tf_op jit(solution)/shard_map/all_to_all | solution.py:75
  163.4 3.9 %all-to-all-done.1 = f32[3,3,2,256]{3,1,0,2:T(4,128)S(1)} async-done(((f32[3,3,2,256]{3,1,0,2:T(4,128)}), f32[3,3,2,256]{3,1,0,2:T(4,128)S(1)}, u32[]{:S(2)}, u32[]{:S(2)}) %all-to-all-start.1) | async-done | bytes 18464 | tf_op jit(solution)/shard_map/all_to_all | solution.py:75
  167.3 0.3 copy.78
  167.6 0.0 slice-done
  167.6 9.5 %scatter_fusion = f32[3,4096]{0,1:T(8,128)S(1)} fusion(f32[3,4096]{0,1:T(8,128)S(1)} %slice-done, s32[1536]{0:T(1024)S(1)} %fusion.5, f32[1536,3]{1,0:T(8,128)S(1)} %copy.78), kind=kCustom, calls=%fused_computation.5 | custom fusion | flops 4608 | bytes 61440 | tf_op jit(solution)/shard_map/scatter-add | solution.py:79
  177.2 0.0 copy-done.4
  177.2 2.0 broadcast_multiply_fusion
  179.1 4.3 %gather_fusion.2 = f32[1536,3]{1,0:T(8,128)S(1)} fusion(f32[3,4096]{0,1:T(8,128)} %broadcast_multiply_fusion, s32[2048]{0:T(1024)S(1)} %pad_clamp_fusion), kind=kCustom, calls=%fused_computation.2 | custom fusion | bytes 43008 | tf_op jit(solution)/shard_map/gather | solution.py:51
  183.5 0.3 copy.79
  183.8 6.3 %all_to_all.15 = f32[3,3,2,256]{3,1,0,2:T(4,128)S(1)} all-to-all(f32[3,3,2,256]{3,1,0,2:T(4,128)S(1)} %broadcast_multiply_fusion.2), channel_id=1, replica_groups=mesh['groups'=2,'dom'=4,'sub'=2,'field'=2] {'sub'}, dimensions={2} | all-to-all | bytes 36864 | tf_op jit(solution)/shard_map/all_to_all | solution.py:52
  190.1 3.4 %collective-permute-start.4 = (f32[3,1,2,256]{3,1,0,2:T(1,128)S(1)}, f32[3,1,2,256]{3,1,0,2:T(1,128)S(1)}, u32[]{:S(2)}, u32[]{:S(2)}) collective-permute-start(f32[3,1,2,256]{3,1,0,2:T(1,128)S(1)} %get-tuple-element.18), channel_id=1, source_target_pairs={{0,4},{4,8},{8,12},{1,5},{5,9},{9,13},{2,6},{6,10},{10,14},{3,7},{... | collective-permute-start | bytes 18440 | tf_op jit(solution)/shard_map/ppermute | solution.py:17
  193.5 1.3 collective-permute-start.5
  194.8 0.0 collective-permute-done.4
  194.8 4.2 %collective-permute-done.5 = f32[3,1,2,256]{3,1,0,2:T(1,128)S(1)} collective-permute-done((f32[3,1,2,256]{3,1,0,2:T(1,128)S(1)}, f32[3,1,2,256]{3,1,0,2:T(1,128)S(1)}, u32[]{:S(2)}, u32[]{:S(2)}) %collective-permute-start.5) | collective-permute-done | bytes 6176 | tf_op jit(solution)/shard_map/ppermute | solution.py:19
  199.1 0.3 copy.83
  199.4 1.7 pad_maximum_fusion
  201.1 36.1 %gather_fusion.3 = f32[10240,3]{1,0:T(8,128)} fusion(f32[3,5632]{0,1:T(8,128)} %pad_maximum_fusion, s32[10240]{0:T(1024)S(1)} %broadcast_clamp_fusion), kind=kCustom, calls=%fused_computation.3 | custom fusion | bytes 286720 | tf_op jit(solution)/shard_map/gather | solution.py:82
  237.2 4.2 %copy.84 = f32[10,1024,3]{1,0,2:T(8,128)S(1)} copy(f32[10,1024,3]{2,1,0:T(8,128)} %bitcast.27) | data formatting | bytes 245760 | tf_op jit(solution)/shard_map/gather | solution.py:82
  241.5 0.0 copy-done.5
  241.5 0.0 copy-done.8
  241.5 0.7 multiply_reduce_fusion.1
  242.2 6.4 %all-reduce = (f32[]{:T(128)}, f32[]{:T(128)}, f32[]{:T(128)}, f32[]{:T(128)}) all-reduce(f32[]{:T(128)} %get-tuple-element.5, f32[]{:T(128)} %get-tuple-element.6, f32[]{:T(128)} %get-tuple-element.4, f32[]{:T(128)} %get-tuple-element.3), channel_id=1, replica_groups=mesh['groups'=2,'dom'=4,'sub'=2,'field'=2] {'sub','field'}, use_global_device_ids=true, to_apply=%region_1.0 | all-reduce | flops 4 | bytes 32 | tf_op jit(solution)/shard_map/psum | solution.py:85
  248.6 10.5 %all-reduce.1 = (f32[]{:T(128)}, f32[]{:T(128)}, f32[]{:T(128)}, f32[]{:T(128)}) all-reduce(f32[]{:T(128)} %get-tuple-element.7, f32[]{:T(128)} %get-tuple-element.8, f32[]{:T(128)} %get-tuple-element.9, f32[]{:T(128)} %get-tuple-element.10), channel_id=1, replica_groups=mesh['groups'=2,'dom'=4,'sub'=2,'field'=2] {'dom'}, use_global_device_ids=true, to_apply=%region_2.0 | all-reduce | flops 4 | bytes 32 | tf_op jit(solution)/shard_map/psum | solution.py:84
  263.1 0.6 multiply_add_fusion
  (38 shorter events, 0.5 us)
Async XLA Ops:
  7.2 63.8 %copy-start = (f32[30,30]{1,0:T(8,128)S(1)}, f32[30,30]{1,0:T(8,128)}, u32[]{:S(2)}) copy-start(f32[30,30]{1,0:T(8,128)} %param.23) | copy-start | bytes 10804
  7.2 24.4 %copy-start.2 = (f32[3,4096]{1,0:T(4,128)S(1)}, f32[3,4096]{1,0:T(4,128)}, u32[]{:S(2)}) copy-start(f32[3,4096]{1,0:T(4,128)} %param.12) | copy-start | bytes 147460
  7.2 10.9 %copy-start.3 = (s32[10,1024]{1,0:T(8,128)S(1)}, s32[10,1024]{1,0:T(8,128)}, u32[]{:S(2)}) copy-start(s32[10,1024]{1,0:T(8,128)} %param.14) | copy-start | bytes 122884
  7.2 20.0 %copy-start.7 = (f32[1024]{0:T(1024)S(1)}, f32[1024]{0:T(1024)}, u32[]{:S(2)}) copy-start(f32[1024]{0:T(1024)} %param.20) | copy-start | bytes 12292
  7.2 20.0 %copy-start.6 = (f32[1024]{0:T(1024)S(1)}, f32[1024]{0:T(1024)}, u32[]{:S(2)}) copy-start(f32[1024]{0:T(1024)} %param.16) | copy-start | bytes 12292
  13.8 8.1 %all-to-all-start = ((f32[3,3,2,256]{3,1,0,2:T(4,128)}), f32[3,3,2,256]{3,1,0,2:T(4,128)S(1)}, u32[]{:S(2)}, u32[]{:S(2)}) async-start(f32[3,3,2,256]{3,1,0,2:T(4,128)} %broadcast_multiply_fusion.4), calls=%async_computation | async-start | bytes 49152 | tf_op jit(solution)/shard_map/all_to_all | solution.py:52
  18.1 130.5 %all-reduce.4.cloned.1.call-start = ((), (), s32[]{:S(2)}) async-start(), calls=%async_computation.3 | async-start | bytes 5767168 | tf_op jit(solution)/shard_map/psum | solution.py:72
  22.0 5.3 %collective-permute-start = (f32[3,1,2,256]{3,1,0,2:T(1,128)S(1)}, f32[3,1,2,256]{3,1,0,2:T(1,128)S(1)}, u32[]{:S(2)}, u32[]{:S(2)}) collective-permute-start(f32[3,1,2,256]{3,1,0,2:T(1,128)S(1)} %get-tuple-element.22), channel_id=1, source_target_pairs={{0,4},{4,8},{8,12},{1,5},{5,9},{9,13},{2,6},{6,10},{10,14},{3,7},{... | collective-permute-start | bytes 18440 | tf_op jit(solution)/shard_map/ppermute | solution.py:17
  25.9 5.5 %collective-permute-start.1 = (f32[3,1,2,256]{3,1,0,2:T(1,128)S(1)}, f32[3,1,2,256]{3,1,0,2:T(1,128)S(1)}, u32[]{:S(2)}, u32[]{:S(2)}) collective-permute-start(f32[3,1,2,256]{3,1,0,2:T(1,128)S(1)} %get-tuple-element.23), channel_id=1, source_target_pairs={{4,0},{8,4},{12,8},{5,1},{9,5},{13,9},{6,2},{10,6},{14,10},{7,3},{... | collective-permute-start | bytes 18440 | tf_op jit(solution)/shard_map/ppermute | solution.py:19
  150.1 17.5 %slice-start = ((f32[3,5632]{0,1:T(8,128)}), f32[3,4096]{0,1:T(8,128)S(1)}, s32[]{:S(2)}) async-start(f32[3,5632]{0,1:T(8,128)} %all-reduce.4.cloned.1.call-done), calls=%async_computation.4 | async-start | bytes 4194304 | tf_op jit(solution)/shard_map/slice | solution.py:77
  150.1 27.1 %copy-start.4 = (f32[4096]{0:T(1024)S(1)}, f32[4096]{0:T(1024)}, u32[]{:S(2)}) copy-start(f32[4096]{0:T(1024)} %param.13) | copy-start | bytes 49156
  150.1 5.1 %collective-permute-start.2 = (f32[3,1,2,256]{3,1,0,2:T(1,128)S(1)}, f32[3,1,2,256]{3,1,0,2:T(1,128)S(1)}, u32[]{:S(2)}, u32[]{:S(2)}) collective-permute-start(f32[3,1,2,256]{3,1,0,2:T(1,128)S(1)} %get-tuple-element.20), channel_id=1, source_target_pairs={{0,4},{4,8},{8,12},{1,5},{5,9},{9,13},{2,6},{6,10},{10,14},{3,7},{... | collective-permute-start | bytes 18440 | tf_op jit(solution)/shard_map/ppermute | solution.py:17
  153.9 5.5 %collective-permute-start.3 = (f32[3,1,2,256]{3,1,0,2:T(1,128)S(1)}, f32[3,1,2,256]{3,1,0,2:T(1,128)S(1)}, u32[]{:S(2)}, u32[]{:S(2)}) collective-permute-start(f32[3,1,2,256]{3,1,0,2:T(1,128)S(1)} %get-tuple-element.21), channel_id=1, source_target_pairs={{4,0},{8,4},{12,8},{5,1},{9,5},{13,9},{6,2},{10,6},{14,10},{7,3},{... | collective-permute-start | bytes 18440 | tf_op jit(solution)/shard_map/ppermute | solution.py:19
  160.1 7.1 %all-to-all-start.1 = ((f32[3,3,2,256]{3,1,0,2:T(4,128)}), f32[3,3,2,256]{3,1,0,2:T(4,128)S(1)}, u32[]{:S(2)}, u32[]{:S(2)}) async-start(f32[3,3,2,256]{3,1,0,2:T(4,128)} %slice.40), calls=%async_computation.1 | async-start | bytes 49152 | tf_op jit(solution)/shard_map/all_to_all | solution.py:75
  179.1 20.2 %copy-start.1 = (f32[3,4096]{0,1:T(8,128)S(1)}, f32[3,4096]{0,1:T(8,128)}, u32[]{:S(2)}) copy-start(f32[3,4096]{0,1:T(8,128)} %broadcast_multiply_fusion) | copy-start | bytes 147460
  190.1 4.7 %collective-permute-start.4 = (f32[3,1,2,256]{3,1,0,2:T(1,128)S(1)}, f32[3,1,2,256]{3,1,0,2:T(1,128)S(1)}, u32[]{:S(2)}, u32[]{:S(2)}) collective-permute-start(f32[3,1,2,256]{3,1,0,2:T(1,128)S(1)} %get-tuple-element.18), channel_id=1, source_target_pairs={{0,4},{4,8},{8,12},{1,5},{5,9},{9,13},{2,6},{6,10},{10,14},{3,7},{... | collective-permute-start | bytes 18440 | tf_op jit(solution)/shard_map/ppermute | solution.py:17
  193.5 5.5 %collective-permute-start.5 = (f32[3,1,2,256]{3,1,0,2:T(1,128)S(1)}, f32[3,1,2,256]{3,1,0,2:T(1,128)S(1)}, u32[]{:S(2)}, u32[]{:S(2)}) collective-permute-start(f32[3,1,2,256]{3,1,0,2:T(1,128)S(1)} %get-tuple-element.19), channel_id=1, source_target_pairs={{4,0},{8,4},{12,8},{5,1},{9,5},{13,9},{6,2},{10,6},{14,10},{7,3},{... | collective-permute-start | bytes 18440 | tf_op jit(solution)/shard_map/ppermute | solution.py:19
  237.2 4.3 %copy-start.5 = (f32[1024]{0:T(1024)S(1)}, f32[1024]{0:T(1024)}, u32[]{:S(2)}) copy-start(f32[1024]{0:T(1024)} %param.19) | copy-start | bytes 12292
  237.2 4.3 %copy-start.8 = (f32[1024]{0:T(1024)S(1)}, f32[1024]{0:T(1024)}, u32[]{:S(2)}) copy-start(f32[1024]{0:T(1024)} %param.17) | copy-start | bytes 12292
  237.2 25.9 %copy-start.9 = (f32[1024]{0:T(1024)S(1)}, f32[1024]{0:T(1024)}, u32[]{:S(2)}) copy-start(f32[1024]{0:T(1024)} %param.18) | copy-start | bytes 12292
Sparse Core Ops, SparseCore 0:
  126.4 22.0 all-reduce.3
